TPU v7x, 32 devices: a whole 2x2x4 slice. The times are simulated.
32 devices in a mesh: energy: 8 (over z, x), slab: 4 (over y, core).
Axes of the slice: x: 2, y: 2, z: 4, core: 2. Of those that a mesh axis runs over, the one named last changes fastest.
Arguments:
- green_blocks: bfloat16 [8, 4, 512, 512], P('energy', 'slab'), may hold values from -6 to 6
- coulomb: bfloat16 [4, 512, 512], P('slab'), may hold values from -0.25 to 0.25
- couple_cols: int32 [4, 128, 8], P('slab'), may hold values from 0 to 127
- couple_vals: bfloat16 [4, 128, 8], P('slab'), may hold values from -0.8984375 to 0.8984375
Outputs:
- new_green: bfloat16 [8, 4, 512, 512], P('energy', 'slab')
Inputs may be any that keep to these rules, and one draw needn't show every extreme that they name: couple_cols[s, i, k] names one of the first 128 orbitals of slab s + 1.
All inputs are finite; a program needn't handle non-finite values.
Results may differ from a plain program's by a relative error of at most 0.015.
Values may be sent and summed in bfloat16 or wider, within the bound.
A program may use at most 64 MiB of HBM per device.

v0:
```python
import functools
import math

import jax
import jax.numpy as jnp
from jax import lax
from jax.experimental import pallas as pl
from jax.experimental.pallas import tpu as pltpu
from jax.sharding import PartitionSpec as P


def from_behind(x, axis, by):
    size = lax.axis_size(axis)
    pairs = [(i, i + by) for i in range(size) if 0 <= i + by < size]
    return lax.ppermute(x, axis, pairs)


def plain_dot(left, right):
    return jnp.dot(left, right, preferred_element_type=jnp.float32)


def split_parts(values):
    upper = values.astype(jnp.bfloat16)
    lower = (values - upper.astype(jnp.float32)).astype(jnp.bfloat16)
    return (upper, lower)


def coupling_matrix(column_ids, coupling_values):
    width = column_ids.shape[0]
    hits = column_ids[:, :, None] == jnp.arange(width, dtype=jnp.int32)[None, None, :]
    summed = jnp.sum(
        jnp.where(hits, coupling_values.astype(jnp.float32)[:, :, None], jnp.float32(0.0)), axis=1
    )
    return summed.astype(jnp.bfloat16)


def on_device(green_blocks, coulomb, couple_cols, couple_vals):
    own_green = green_blocks[:, 0]
    coulomb_block = coulomb[0]
    per_device = own_green.shape[0]
    orbitals = own_green.shape[1]
    volume = lax.axis_size("energy")
    energies = per_device * volume
    inv_root = 1.0 / math.sqrt(orbitals)
    flipped = jnp.swapaxes(own_green, 1, 2)
    received, flipped_recv = (
        lax.all_to_all(own_green, "energy", split_axis=1, concat_axis=0, tiled=True),
        lax.all_to_all(flipped, "energy", split_axis=1, concat_axis=0, tiled=True),
    )
    green_entries = received.reshape(energies, -1)
    flipped_entries = flipped_recv.reshape(energies, -1)
    entry_shape = received.shape
    halfway = energies // 2 + 1
    frequency = jnp.arange(halfway, dtype=jnp.int32)
    energy_index = jnp.arange(energies, dtype=jnp.int32)
    angles = (frequency[:, None] * energy_index[None, :] % energies).astype(jnp.float32) * (
        2.0 * math.pi / energies
    )
    cosine = jnp.cos(angles)
    sine = jnp.sin(angles)
    weights = (
        jnp.where((frequency == 0) | (2 * frequency == energies), 1.0, 2.0).astype(jnp.float32)
        / energies
    )
    forward_high, forward_low = split_parts(jnp.concatenate([cosine, -sine], axis=0))
    backward_table = jnp.concatenate(
        [cosine * weights[:, None], -sine * weights[:, None]], axis=0
    ).T
    backward_high, backward_low = split_parts(backward_table)

    def spectrum(entries):
        stacked = plain_dot(forward_high, entries) + plain_dot(forward_low, entries)
        return (stacked[:halfway], stacked[halfway:])

    def to_values(real_part, imag_part):
        data_high, data_low = split_parts(jnp.concatenate([real_part, imag_part], axis=0))
        return (
            plain_dot(backward_high, data_high)
            + plain_dot(backward_high, data_low)
            + plain_dot(backward_low, data_high)
        )

    green_real, green_imag = spectrum(green_entries)
    mirror_real, mirror_imag = spectrum(flipped_entries)
    polar_entries = to_values(
        green_real * mirror_real + green_imag * mirror_imag,
        green_imag * mirror_real - green_real * mirror_imag,
    )
    polar_entries = (polar_entries * (0.5 / math.sqrt(orbitals * energies))).astype(jnp.bfloat16)
    polar = lax.all_to_all(
        polar_entries.reshape(entry_shape), "energy", split_axis=0, concat_axis=1, tiled=True
    )
    inner = jnp.einsum(
        "ij,ejk->eik", coulomb_block, polar, preferred_element_type=jnp.float32
    ).astype(jnp.bfloat16)
    second = jnp.einsum("eij,jk->eik", inner, coulomb_block, preferred_element_type=jnp.float32)
    third = jnp.einsum(
        "eij,ejk->eik", inner, second.astype(jnp.bfloat16), preferred_element_type=jnp.float32
    )
    screened = (coulomb_block.astype(jnp.float32)[None] + second + third).astype(jnp.bfloat16)
    screened_entries = lax.all_to_all(
        screened, "energy", split_axis=1, concat_axis=0, tiled=True
    ).reshape(energies, -1)
    screen_real, screen_imag = spectrum(screened_entries)
    sigma_entries = to_values(
        green_real * screen_real - green_imag * screen_imag,
        green_real * screen_imag + green_imag * screen_real,
    )
    sigma_entries = (sigma_entries * (0.2 / math.sqrt(energies))).astype(jnp.bfloat16)
    sigma = lax.all_to_all(
        sigma_entries.reshape(entry_shape), "energy", split_axis=0, concat_axis=1, tiled=True
    )
    interface = couple_cols.shape[1]
    last = orbitals - interface
    coupling = coupling_matrix(couple_cols[0], couple_vals[0])
    prev_green, previous = from_behind((own_green, coupling), "slab", 1)
    next_green = from_behind(own_green, "slab", -1)
    prev_corner = prev_green[:, last:, last:]
    next_corner = next_green[:, :interface, :interface]
    near_next = jnp.einsum(
        "ij,ejk->eik", coupling, next_corner, preferred_element_type=jnp.float32
    ).astype(jnp.bfloat16)
    near_prev = jnp.einsum(
        "ji,ejk->eik", previous, prev_corner, preferred_element_type=jnp.float32
    ).astype(jnp.bfloat16)
    right_part = (
        jnp.einsum("eij,kj->eik", near_next, coupling, preferred_element_type=jnp.float32)
        * inv_root
    )
    left_part = (
        jnp.einsum("eij,jk->eik", near_prev, previous, preferred_element_type=jnp.float32)
        * inv_root
    )
    total = sigma.astype(jnp.float32)
    total = total.at[:, last:, last:].add(right_part)
    total = total.at[:, :interface, :interface].add(left_part)
    total_b = total.astype(jnp.bfloat16)
    dressed = jnp.einsum(
        "eij,ejk->eik", own_green, total_b, preferred_element_type=jnp.float32
    ).astype(jnp.bfloat16)
    updated = (
        own_green
        + jnp.einsum("eij,ejk->eik", dressed, own_green, preferred_element_type=jnp.float32)
        * inv_root
    )
    return updated.astype(jnp.bfloat16)[:, None]


MESH = pl.DeviceIdType.MESH


def unit_blocks(unit, grid):
    odd = grid - 1
    paired = grid * odd // 2
    slot = unit // odd
    turn = unit % odd
    diagonal = unit // paired
    first = (turn + slot) % odd
    second = (turn + odd - slot) % odd
    lone = 1 - (slot + odd - 1) // odd
    row = lone * odd + (1 - lone) * first
    col = lone * turn + (1 - lone) * second
    corner = 2 * (unit - paired)
    row0 = diagonal * corner + (1 - diagonal) * row
    col0 = diagonal * corner + (1 - diagonal) * col
    row1 = diagonal * (corner + 1) + (1 - diagonal) * col
    col1 = diagonal * (corner + 1) + (1 - diagonal) * row
    return ((row0, col0), (row1, col1))


def fused_kernel(
    volume, slabs, grid, scale_polar, scale_sigma, inv_root,
    green_hbm, coulomb_hbm, cols_hbm, vals_hbm, out,
    green, coulomb, cols, vals,
    green_in, mirror, polar_out, polar_in, matrix, inner, screened, screen_in, sigma_out, sigma_in,
    coupling, turned, next_corner, left_out, left_in, right_in, total,
    send_sem, recv_sem, slab_send, slab_recv, load_sem,
):
    loads = [
        pltpu.make_async_copy(source, target, load_sem.at[n])
        for n, (source, target) in enumerate(
            ((green_hbm, green), (coulomb_hbm, coulomb), (cols_hbm, cols), (vals_hbm, vals))
        )
    ]
    for load in loads:
        load.start()
    me = lax.axis_index("energy")
    slab = lax.axis_index("slab")
    size = green.shape[0] // grid
    last = green.shape[0] - size
    order = sorted(range(1, volume), key=lambda k: (-min(k, volume - k), k))
    has_prev = 1 - (slabs - 1 - slab + 0) // (slabs - 1)
    has_next = 1 - slab // (slabs - 1)
    diagonal = me // (grid * (grid - 1) // 2)

    def peer_of(k):
        return lax.rem(me + k, volume)

    barrier = pltpu.get_barrier_semaphore()
    for k in range(1, volume):
        pl.semaphore_signal(barrier, inc=1, device_id=(peer_of(k), slab), device_id_type=MESH)

    @pl.when(slab > 0)
    def _():
        pl.semaphore_signal(barrier, inc=1, device_id=(me, slab - 1), device_id_type=MESH)

    @pl.when(slab < slabs - 1)
    def _():
        pl.semaphore_signal(barrier, inc=1, device_id=(me, slab + 1), device_id_type=MESH)

    pl.semaphore_wait(barrier, volume - 1 + has_prev + has_next)

    def block_of(ref, coords):
        row = pl.multiple_of(coords[0] * size, size)
        col = pl.multiple_of(coords[1] * size, size)
        return ref.at[pl.ds(row, size), pl.ds(col, size)]

    def remote(src, dst, phase, k, half):
        return pltpu.make_async_remote_copy(
            src_ref=src, dst_ref=dst,
            send_sem=send_sem.at[phase, k, half], recv_sem=recv_sem.at[phase, k, half],
            device_id=(peer_of(k), slab), device_id_type=MESH,
        )

    def scatter(source, landing, phase):
        copies = []
        for half in range(2):
            for k in order:
                coords = unit_blocks(peer_of(k), grid)
                copy = remote(block_of(source, coords[half]), landing.at[me, half], phase, k, half)
                copy.start()
                copies.append(copy)
        own = unit_blocks(me, grid)
        for half in range(2):
            landing[me, half] = block_of(source, own[half])[...]
        return copies

    def gather(source, landing, phase, half):
        copies = []
        for k in order:
            copy = remote(source.at[peer_of(k), half], landing.at[me, half], phase, k, half)
            copy.start()
            copies.append(copy)
        landing[me, half] = source[me, half]
        return copies

    def arrived(copies):
        for copy in copies:
            copy.wait_recv()

    def from_of(k):
        return lax.rem(me + volume - k, volume)

    def place(landing, target, source, half):
        block_of(target, unit_blocks(source, grid)[half])[...] = landing[source, half]

    def assemble(landing, target, copies, half):
        place(landing, target, me, half)
        for k, copy in zip(order, copies):
            copy.wait_recv()
            place(landing, target, from_of(k), half)

    loads[0].wait()
    sent = scatter(green, green_in, 0)
    corner_copy = pltpu.make_async_remote_copy(
        src_ref=green.at[pl.ds(0, size), pl.ds(0, size)], dst_ref=next_corner,
        send_sem=slab_send.at[0], recv_sem=slab_recv.at[0],
        device_id=(me, slab - has_prev), device_id_type=MESH,
    )
    left_copy = pltpu.make_async_remote_copy(
        src_ref=left_out, dst_ref=left_in,
        send_sem=slab_send.at[1], recv_sem=slab_recv.at[1],
        device_id=(me, slab + has_next), device_id_type=MESH,
    )

    @pl.when(slab > 0)
    def _():
        corner_copy.start()

    loads[2].wait()
    loads[3].wait()
    ids = cols[...]
    values = vals[...].astype(jnp.float32)
    columns = lax.broadcasted_iota(jnp.int32, (size, size), 0)
    summed = jnp.zeros((size, size), jnp.float32)
    for k in range(ids.shape[0]):
        summed += jnp.where(ids[k:k + 1, :] == columns, values[k:k + 1, :], jnp.float32(0.0))
    summed = summed.astype(jnp.bfloat16).astype(jnp.float32)
    turned[...] = summed.astype(jnp.bfloat16)
    coupling[...] = summed.T.astype(jnp.bfloat16)

    @pl.when(slab < slabs - 1)
    def _():
        near_prev = plain_dot(turned[...], green[last:, last:]).astype(jnp.bfloat16)
        left_out[...] = plain_dot(near_prev, coupling[...]) * inv_root
        left_copy.start()

    everything = list(sent)
    rows_at_once = 16

    def flip(e, half):
        to = diagonal * half + (1 - diagonal) * (1 - half)
        mirror[e, to] = green_in[e, half].astype(jnp.float32).T

    for half in range(2):
        flip(me, half)
        for k, copy in zip(order, sent[half * len(order):]):
            copy.wait_recv()
            flip(from_of(k), half)

    polar_copies = []
    for half in range(2):
        def correlate(step, carry, half=half):
            rows = pl.ds(pl.multiple_of(step * rows_at_once, rows_at_once), rows_at_once)
            mine = [green_in[e, half, rows, :].astype(jnp.float32) for e in range(volume)]
            theirs = [mirror[e, half, rows, :] for e in range(volume)]
            for e in range(volume):
                acc = mine[0] * theirs[(0 - e) % volume]
                for e2 in range(1, volume):
                    acc += mine[e2] * theirs[(e2 - e) % volume]
                polar_out[e, half, rows, :] = (acc * scale_polar).astype(jnp.bfloat16)
            return carry

        lax.fori_loop(0, size // rows_at_once, correlate, 0)
        copies = gather(polar_out, polar_in, 1, half)
        everything += copies
        polar_copies.append(copies)
    loads[1].wait()
    for half in range(2):
        assemble(polar_in, matrix, polar_copies[half], half)
    inner[...] = plain_dot(coulomb[...], matrix[...]).astype(jnp.bfloat16)
    second = plain_dot(inner[...], coulomb[...])
    total[...] = second
    matrix[...] = second.astype(jnp.bfloat16)
    third = plain_dot(inner[...], matrix[...])
    screened[...] = (coulomb[...].astype(jnp.float32) + total[...] + third).astype(jnp.bfloat16)
    copies = scatter(screened, screen_in, 2)
    everything += copies
    waves = copies

    sigma_copies = []
    for half in range(2):
        arrived(waves[half * len(order):(half + 1) * len(order)])

        def convolve(step, carry, half=half):
            rows = pl.ds(pl.multiple_of(step * rows_at_once, rows_at_once), rows_at_once)
            mine = [green_in[e, half, rows, :].astype(jnp.float32) for e in range(volume)]
            waves = [screen_in[e, half, rows, :].astype(jnp.float32) for e in range(volume)]
            for e in range(volume):
                acc = mine[0] * waves[e]
                for e2 in range(1, volume):
                    acc += mine[e2] * waves[(e - e2) % volume]
                sigma_out[e, half, rows, :] = (acc * scale_sigma).astype(jnp.bfloat16)
            return carry

        lax.fori_loop(0, size // rows_at_once, convolve, 0)
        copies = gather(sigma_out, sigma_in, 3, half)
        everything += copies
        sigma_copies.append(copies)

    @pl.when(slab < slabs - 1)
    def _():
        corner_copy.wait_recv()
        near_next = plain_dot(coupling[...], next_corner[...]).astype(jnp.bfloat16)
        right_in[...] = plain_dot(near_next, turned[...]) * inv_root

    for half in range(2):
        assemble(sigma_in, matrix, sigma_copies[half], half)

    @pl.when(slab < slabs - 1)
    def _():
        matrix[last:, last:] = (matrix[last:, last:].astype(jnp.float32) + right_in[...]).astype(jnp.bfloat16)
        left_copy.wait_send()

    @pl.when(slab > 0)
    def _():
        left_copy.wait_recv()
        matrix[:size, :size] = (matrix[:size, :size].astype(jnp.float32) + left_in[...]).astype(jnp.bfloat16)
        corner_copy.wait_send()

    inner[...] = plain_dot(green[...], matrix[...]).astype(jnp.bfloat16)
    updated = green[...].astype(jnp.float32) + plain_dot(inner[...], green[...]) * inv_root
    out[...] = updated.astype(jnp.bfloat16)
    for copy in everything:
        copy.wait_send()


def fused_on_device(grid, green_blocks, coulomb, couple_cols, couple_vals):
    volume = lax.axis_size("energy")
    slabs = lax.axis_size("slab")
    orbitals = green_blocks.shape[-1]
    size = orbitals // grid
    half_type = jnp.bfloat16
    pieces = pltpu.VMEM((volume, 2, size, size), half_type)
    whole = pltpu.VMEM((orbitals, orbitals), half_type)
    block = pltpu.VMEM((size, size), half_type)
    wide = pltpu.VMEM((size, size), jnp.float32)
    result = pl.pallas_call(
        functools.partial(
            fused_kernel, volume, slabs, grid,
            0.5 / math.sqrt(orbitals * volume), 0.2 / math.sqrt(volume), 1.0 / math.sqrt(orbitals),
        ),
        out_shape=jax.ShapeDtypeStruct((orbitals, orbitals), half_type),
        in_specs=[pl.BlockSpec(memory_space=pltpu.HBM)] * 4,
        out_specs=pl.BlockSpec(memory_space=pltpu.VMEM),
        scratch_shapes=[
            whole, whole, pltpu.VMEM(couple_cols.shape[:0:-1], jnp.int32), pltpu.VMEM(couple_vals.shape[:0:-1], half_type),
            pieces, pltpu.VMEM((volume, 2, size, size), jnp.float32), pieces, pieces,
            whole, whole, whole, pieces, pieces, pieces,
            block, block, block, wide, wide, wide, pltpu.VMEM((orbitals, orbitals), jnp.float32),
            pltpu.SemaphoreType.DMA((4, volume, 2)), pltpu.SemaphoreType.DMA((4, volume, 2)),
            pltpu.SemaphoreType.DMA((2,)), pltpu.SemaphoreType.DMA((2,)), pltpu.SemaphoreType.DMA((4,)),
        ],
        compiler_params=pltpu.CompilerParams(
            collective_id=0, has_side_effects=True, vmem_limit_bytes=67043328
        ),
    )(green_blocks[0, 0], coulomb[0], couple_cols[0].T, couple_vals[0].T)
    return result[None, None]


def fused_grid(mesh):
    volume = mesh.shape["energy"]
    grid = math.isqrt(2 * volume)
    return grid if grid * grid == 2 * volume and grid % 2 == 0 else 0


def on_any(grid, green_blocks, coulomb, couple_cols, couple_vals):
    orbitals = green_blocks.shape[-1]
    fits = (
        grid > 0
        and green_blocks.shape[:2] == (1, 1)
        and orbitals % (128 * max(grid, 1)) == 0
        and couple_cols.shape[1] * grid == orbitals
        and lax.axis_size("slab") > 1
    )
    if fits:
        return fused_on_device(grid, green_blocks, coulomb, couple_cols, couple_vals)
    return on_device(green_blocks, coulomb, couple_cols, couple_vals)


def solution(mesh):
    return jax.shard_map(
        functools.partial(on_any, fused_grid(mesh)),
        mesh=mesh,
        in_specs=(
            P("energy", "slab", None, None),
            P("slab", None, None),
            P("slab", None, None),
            P("slab", None, None),
        ),
        out_specs=P("energy", "slab", None, None),
        check_vma=False,
    )
```

profile of v0, /device:TPU:0, one launch (start us, length us, event | category | flops | bytes accessed | tf_op | source)
XLA Modules:
  0.0 59.9 jit_solution(12630749034274063863)
XLA Ops:
  0.0 58.0 %shard_map.46 = bf16[512,512]{1,0:T(8,128)(2,1)} custom-call(bf16[512,512]{1,0:T(8,128)(2,1)} %bitcast.10, bf16[512,512]{1,0:T(8,128)(2,1)} %bitcast.11, s32[8,128]{1,0:T(8,128)} %bitcast.12, bf16[8,128]{1,0:T(8,128)(2,1)} %bitcast.13), custom_call_target="tpu_custom_call" | custom-call | tf_op jit(solution)/shard_map/pallas_call | solution.py:398
  58.0 1.9 %copy.6 = bf16[1,1,512,512]{3,2,1,0:T(8,128)(2,1)} copy(bf16[1,1,512,512]{3,2,1,0:T(8,128)(2,1)} %bitcast.9) | data formatting | bytes 1048576
where the time goes:
time: 60.7 us; the launch traced here: 59.9 us
  Pallas kernels  58 us (96%)
  local copies, waits for them, and re-layouts  1.87 us (3%)
    pallas_call x1, Pallas kernels, fused_on_device(): pl.pallas_call(functools.partial(fused_kernel, volume, slabs, grid, 0.5 /...  58 us
    unnamed x1, local copies, waits for them, and re-layouts  1.87 us

commit v1 on v0

--- a/solution.py
+++ b/solution.py
@@ -168,13 +168,18 @@
     return ((row0, col0), (row1, col1))
 
 
+CHUNKS = 2
+
+
 def fused_kernel(
     volume, slabs, grid, scale_polar, scale_sigma, inv_root,
     green_hbm, coulomb_hbm, cols_hbm, vals_hbm, out,
     green, coulomb, cols, vals,
-    green_in, mirror, polar_out, polar_in, matrix, inner, screened, screen_in, sigma_out, sigma_in,
-    coupling, turned, next_corner, left_out, left_in, right_in, total,
-    send_sem, recv_sem, slab_send, slab_recv, load_sem,
+    stage, landed, mirror, second_half, polar_out, polar_more, matrix, inner, second, screened,
+    screen_in, sigma_out, sigma,
+    coupling, turned, next_corner, left_out, left_in, right_in,
+    g_send, g_recv, p_send, p_recv, m_send, m_recv, w_send, w_recv, s_send, s_recv,
+    slab_send, slab_recv, load_sem,
 ):
     loads = [
         pltpu.make_async_copy(source, target, load_sem.at[n])
@@ -188,13 +193,22 @@
     slab = lax.axis_index("slab")
     size = green.shape[0] // grid
     last = green.shape[0] - size
+    classes = volume // 2
+    paired = grid * (grid - 1) // 2
     order = sorted(range(1, volume), key=lambda k: (-min(k, volume - k), k))
     has_prev = 1 - (slabs - 1 - slab + 0) // (slabs - 1)
     has_next = 1 - slab // (slabs - 1)
-    diagonal = me // (grid * (grid - 1) // 2)
+    diagonal = me // paired
+    my_class = lax.rem(me, classes)
+    first_mate = me - my_class
+    own_blocks = unit_blocks(me, grid)
+    chunk_rows = size // CHUNKS
 
     def peer_of(k):
         return lax.rem(me + k, volume)
+
+    def from_of(k):
+        return lax.rem(me + volume - k, volume)
 
     barrier = pltpu.get_barrier_semaphore()
     for k in range(1, volume):
@@ -208,60 +222,56 @@
     def _():
         pl.semaphore_signal(barrier, inc=1, device_id=(me, slab + 1), device_id_type=MESH)
 
+    def flipped(block):
+        return block.astype(jnp.float32).T.astype(jnp.bfloat16)
+
+    def region(coords, start=0, rows=None):
+        rows = size if rows is None else rows
+        row = pl.multiple_of(coords[0] * size + start, rows)
+        col = pl.multiple_of(coords[1] * size, size)
+        return pl.ds(row, rows), pl.ds(col, size)
+
+    def block_of(ref, coords, start=0, rows=None):
+        return ref.at[region(coords, start, rows)]
+
+    def remote(src, dst, sends, recvs, device):
+        return pltpu.make_async_remote_copy(
+            src_ref=src, dst_ref=dst, send_sem=sends, recv_sem=recvs,
+            device_id=(device, slab), device_id_type=MESH,
+        )
+
+    loads[0].wait()
+    for unit in range(volume):
+        coords = unit_blocks(unit, grid)[1]
+        block = green[coords[0] * size:(coords[0] + 1) * size, coords[1] * size:(coords[1] + 1) * size]
+        stage[unit] = block if unit >= paired else flipped(block)
+
     pl.semaphore_wait(barrier, volume - 1 + has_prev + has_next)
 
-    def block_of(ref, coords):
-        row = pl.multiple_of(coords[0] * size, size)
-        col = pl.multiple_of(coords[1] * size, size)
-        return ref.at[pl.ds(row, size), pl.ds(col, size)]
-
-    def remote(src, dst, phase, k, half):
-        return pltpu.make_async_remote_copy(
-            src_ref=src, dst_ref=dst,
-            send_sem=send_sem.at[phase, k, half], recv_sem=recv_sem.at[phase, k, half],
-            device_id=(peer_of(k), slab), device_id_type=MESH,
-        )
-
-    def scatter(source, landing, phase):
-        copies = []
-        for half in range(2):
+    def span(chunk):
+        return pl.ds(chunk * chunk_rows, chunk_rows)
+
+    green_copies = []
+    for chunk in range(CHUNKS):
+        batch = []
+        for slot in range(2):
             for k in order:
-                coords = unit_blocks(peer_of(k), grid)
-                copy = remote(block_of(source, coords[half]), landing.at[me, half], phase, k, half)
+                peer = peer_of(k)
+                coords = unit_blocks(peer, grid)[0]
+                if slot == 0:
+                    source = block_of(green, coords, chunk * chunk_rows, chunk_rows)
+                else:
+                    source = stage.at[peer, span(chunk)]
+                copy = remote(
+                    source, landed.at[me, slot, span(chunk)],
+                    g_send.at[k, chunk, slot], g_recv.at[k, chunk, slot], peer,
+                )
                 copy.start()
-                copies.append(copy)
-        own = unit_blocks(me, grid)
-        for half in range(2):
-            landing[me, half] = block_of(source, own[half])[...]
-        return copies
-
-    def gather(source, landing, phase, half):
-        copies = []
-        for k in order:
-            copy = remote(source.at[peer_of(k), half], landing.at[me, half], phase, k, half)
-            copy.start()
-            copies.append(copy)
-        landing[me, half] = source[me, half]
-        return copies
-
-    def arrived(copies):
-        for copy in copies:
-            copy.wait_recv()
-
-    def from_of(k):
-        return lax.rem(me + volume - k, volume)
-
-    def place(landing, target, source, half):
-        block_of(target, unit_blocks(source, grid)[half])[...] = landing[source, half]
-
-    def assemble(landing, target, copies, half):
-        place(landing, target, me, half)
-        for k, copy in zip(order, copies):
-            copy.wait_recv()
-            place(landing, target, from_of(k), half)
-
-    loads[0].wait()
-    sent = scatter(green, green_in, 0)
+                batch.append(copy)
+        green_copies.append(batch)
+    landed[me, 0] = block_of(green, own_blocks[0])[...]
+    landed[me, 1] = stage[me]
+
     corner_copy = pltpu.make_async_remote_copy(
         src_ref=green.at[pl.ds(0, size), pl.ds(0, size)], dst_ref=next_corner,
         send_sem=slab_send.at[0], recv_sem=slab_recv.at[0],
@@ -295,57 +305,193 @@
         left_out[...] = plain_dot(near_prev, coupling[...]) * inv_root
         left_copy.start()
 
-    everything = list(sent)
+    loads[1].wait()
     rows_at_once = 16
-
-    def flip(e, half):
-        to = diagonal * half + (1 - diagonal) * (1 - half)
-        mirror[e, to] = green_in[e, half].astype(jnp.float32).T
-
+    steps = chunk_rows // rows_at_once
+
+    def rows_of(step):
+        return pl.ds(pl.multiple_of(step * rows_at_once, rows_at_once), rows_at_once)
+
+    def correlation(mine, theirs, e):
+        acc = mine[0] * theirs[(0 - e) % volume]
+        for e2 in range(1, volume):
+            acc += mine[e2] * theirs[(e2 - e) % volume]
+        return (acc * scale_polar).astype(jnp.bfloat16)
+
+    where = (
+        (0, own_blocks[0]),
+        (1 - diagonal, tuple(
+            diagonal * d + (1 - diagonal) * o for d, o in zip(own_blocks[1], own_blocks[0])
+        )),
+    )
+
+    def polar_copy(k, chunk, slot):
+        peer = peer_of(k)
+        index, coords = where[slot]
+        return remote(
+            polar_out.at[lax.rem(peer, classes), slot, span(chunk)],
+            block_of(matrix.at[index], coords, chunk * chunk_rows, chunk_rows),
+            p_send.at[k, chunk, slot], p_recv.at[k, chunk, slot], peer,
+        )
+
+    def send_polar(chunk):
+        for slot in range(2):
+            for k in order:
+                polar_copy(k, chunk, slot).start()
+
+    def more_copy(target, slot):
+        return remote(
+            polar_more.at[slot],
+            block_of(matrix.at[1], own_blocks[slot]),
+            m_send.at[target, slot], m_recv.at[lax.rem(me, paired), slot], target * classes,
+        )
+
+    def arrived(copies):
+        for copy in copies:
+            copy.wait_recv()
+
+    @pl.when(diagonal == 0)
+    def _():
+        for chunk in range(CHUNKS):
+            arrived(green_copies[chunk])
+
+            def correlate(step, carry):
+                rows = rows_of(step)
+                mine = [landed[e, 0, rows, :].astype(jnp.float32) for e in range(volume)]
+                theirs = [landed[e, 1, rows, :].astype(jnp.float32) for e in range(volume)]
+                for e in range(volume):
+                    if e % classes == 0:
+                        place = (0, e // classes)
+                    else:
+                        place = (min(e, volume - e), e // classes)
+                    polar_out[place[0], place[1], rows, :] = correlation(mine, theirs, e)
+                return carry
+
+            lax.fori_loop(chunk * steps, (chunk + 1) * steps, correlate, 0)
+            send_polar(chunk)
+
+    @pl.when(diagonal == 1)
+    def _():
+        def flip_both(e):
+            for slot in range(2):
+                mirror[e, slot] = flipped(landed[e, slot])
+
+        flip_both(me)
+        for n, k in enumerate(order):
+            for batch in green_copies:
+                for slot in range(2):
+                    batch[slot * len(order) + n].wait_recv()
+            flip_both(from_of(k))
+
+        for slot in range(2):
+            def correlate(step, carry, slot=slot):
+                rows = rows_of(step)
+                mine = [landed[e, slot, rows, :].astype(jnp.float32) for e in range(volume)]
+                theirs = [mirror[e, slot, rows, :].astype(jnp.float32) for e in range(volume)]
+                for e in range(classes):
+                    polar_out[e, slot, rows, :] = correlation(mine, theirs, e)
+                polar_more[slot, rows, :] = correlation(mine, theirs, classes)
+                return carry
+
+            lax.fori_loop(0, size // rows_at_once, correlate, 0)
+        for chunk in range(CHUNKS):
+            send_polar(chunk)
+        for target in range(2):
+            for slot in range(2):
+                more_copy(target, slot).start()
+
+    for slot in range(2):
+        index, coords = where[slot]
+        block_of(matrix.at[index], coords)[...] = polar_out[my_class, slot]
+
+    @pl.when(diagonal == 0)
+    def _():
+        for e in range(volume):
+            second_half[e] = flipped(landed[e, 1])
+
+    @pl.when(diagonal == 1)
+    def _():
+        for e in range(volume):
+            second_half[e] = landed[e, 1]
+
+    swapped = 1 - lax.rem(my_class + classes - 1, classes) // (classes - 1)
+
+    def complete(unit):
+        coords = unit_blocks(unit, grid)
+        off = 1 - unit // paired
+
+        @pl.when(off == 1)
+        def _():
+            for index in range(2):
+                source = swapped * (1 - index) + (1 - swapped) * index
+                block_of(matrix.at[index], coords[1])[...] = flipped(
+                    block_of(matrix.at[source], coords[0])[...]
+                )
+
+        @pl.when(jnp.logical_and(off == 0, my_class > 0))
+        def _():
+            for slot in range(2):
+                block_of(matrix.at[1], coords[slot])[...] = flipped(
+                    block_of(matrix.at[0], coords[slot])[...]
+                )
+
+    complete(me)
+    for k in order:
+        for chunk in range(CHUNKS):
+            for slot in range(2):
+                polar_copy(k, chunk, slot).wait_recv()
+        complete(from_of(k))
+
+    @pl.when(my_class == 0)
+    def _():
+        for unit in range(paired, volume):
+            for slot in range(2):
+                remote(
+                    polar_more.at[slot], block_of(matrix.at[1], unit_blocks(unit, grid)[slot]),
+                    m_send.at[0, slot], m_recv.at[unit - paired, slot], first_mate,
+                ).wait_recv()
+
+    for index in range(2):
+        inner[index] = plain_dot(coulomb[...], matrix[index]).astype(jnp.bfloat16)
+    for index in range(2):
+        product = plain_dot(inner[index], coulomb[...])
+        second[index] = product
+        matrix[index] = product.astype(jnp.bfloat16)
+    for index in range(2):
+        third = plain_dot(inner[index], matrix[index])
+        screened[index] = (coulomb[...].astype(jnp.float32) + second[index] + third).astype(jnp.bfloat16)
+
+    wave_copies = []
     for half in range(2):
-        flip(me, half)
-        for k, copy in zip(order, sent[half * len(order):]):
-            copy.wait_recv()
-            flip(from_of(k), half)
-
-    polar_copies = []
+        batch = []
+        for t in range(1, classes):
+            mate = first_mate + lax.rem(my_class + t, classes)
+            rows, width = region(unit_blocks(mate, grid)[half])
+            copy = remote(
+                screened.at[:, rows, width], screen_in.at[my_class, half],
+                w_send.at[t, half], w_recv.at[t, half], mate,
+            )
+            copy.start()
+            batch.append(copy)
+        wave_copies.append(batch)
     for half in range(2):
-        def correlate(step, carry, half=half):
-            rows = pl.ds(pl.multiple_of(step * rows_at_once, rows_at_once), rows_at_once)
-            mine = [green_in[e, half, rows, :].astype(jnp.float32) for e in range(volume)]
-            theirs = [mirror[e, half, rows, :] for e in range(volume)]
-            for e in range(volume):
-                acc = mine[0] * theirs[(0 - e) % volume]
-                for e2 in range(1, volume):
-                    acc += mine[e2] * theirs[(e2 - e) % volume]
-                polar_out[e, half, rows, :] = (acc * scale_polar).astype(jnp.bfloat16)
-            return carry
-
-        lax.fori_loop(0, size // rows_at_once, correlate, 0)
-        copies = gather(polar_out, polar_in, 1, half)
-        everything += copies
-        polar_copies.append(copies)
-    loads[1].wait()
-    for half in range(2):
-        assemble(polar_in, matrix, polar_copies[half], half)
-    inner[...] = plain_dot(coulomb[...], matrix[...]).astype(jnp.bfloat16)
-    second = plain_dot(inner[...], coulomb[...])
-    total[...] = second
-    matrix[...] = second.astype(jnp.bfloat16)
-    third = plain_dot(inner[...], matrix[...])
-    screened[...] = (coulomb[...].astype(jnp.float32) + total[...] + third).astype(jnp.bfloat16)
-    copies = scatter(screened, screen_in, 2)
-    everything += copies
-    waves = copies
+        rows, width = region(own_blocks[half])
+        screen_in[my_class, half] = screened[:, rows, width]
 
     sigma_copies = []
     for half in range(2):
-        arrived(waves[half * len(order):(half + 1) * len(order)])
+        arrived(wave_copies[half])
 
         def convolve(step, carry, half=half):
-            rows = pl.ds(pl.multiple_of(step * rows_at_once, rows_at_once), rows_at_once)
-            mine = [green_in[e, half, rows, :].astype(jnp.float32) for e in range(volume)]
-            waves = [screen_in[e, half, rows, :].astype(jnp.float32) for e in range(volume)]
+            rows = rows_of(step)
+            if half == 0:
+                mine = [landed[e, 0, rows, :].astype(jnp.float32) for e in range(volume)]
+            else:
+                mine = [second_half[e, rows, :].astype(jnp.float32) for e in range(volume)]
+            waves = [
+                screen_in[min(e, volume - e) % classes, half, e // classes, rows, :].astype(jnp.float32)
+                for e in range(volume)
+            ]
             for e in range(volume):
                 acc = mine[0] * waves[e]
                 for e2 in range(1, volume):
@@ -354,9 +500,15 @@
             return carry
 
         lax.fori_loop(0, size // rows_at_once, convolve, 0)
-        copies = gather(sigma_out, sigma_in, 3, half)
-        everything += copies
-        sigma_copies.append(copies)
+        for k in order:
+            peer = peer_of(k)
+            copy = remote(
+                sigma_out.at[peer, half], block_of(sigma, own_blocks[half]),
+                s_send.at[k, half], s_recv.at[k, half], peer,
+            )
+            copy.start()
+            sigma_copies.append(copy)
+        block_of(sigma, own_blocks[half])[...] = sigma_out[me, half]
 
     @pl.when(slab < slabs - 1)
     def _():
@@ -364,25 +516,35 @@
         near_next = plain_dot(coupling[...], next_corner[...]).astype(jnp.bfloat16)
         right_in[...] = plain_dot(near_next, turned[...]) * inv_root
 
-    for half in range(2):
-        assemble(sigma_in, matrix, sigma_copies[half], half)
+    arrived(sigma_copies)
 
     @pl.when(slab < slabs - 1)
     def _():
-        matrix[last:, last:] = (matrix[last:, last:].astype(jnp.float32) + right_in[...]).astype(jnp.bfloat16)
+        sigma[last:, last:] = (sigma[last:, last:].astype(jnp.float32) + right_in[...]).astype(jnp.bfloat16)
         left_copy.wait_send()
 
     @pl.when(slab > 0)
     def _():
         left_copy.wait_recv()
-        matrix[:size, :size] = (matrix[:size, :size].astype(jnp.float32) + left_in[...]).astype(jnp.bfloat16)
+        sigma[:size, :size] = (sigma[:size, :size].astype(jnp.float32) + left_in[...]).astype(jnp.bfloat16)
         corner_copy.wait_send()
 
-    inner[...] = plain_dot(green[...], matrix[...]).astype(jnp.bfloat16)
-    updated = green[...].astype(jnp.float32) + plain_dot(inner[...], green[...]) * inv_root
+    inner[0] = plain_dot(green[...], sigma[...]).astype(jnp.bfloat16)
+    updated = green[...].astype(jnp.float32) + plain_dot(inner[0], green[...]) * inv_root
     out[...] = updated.astype(jnp.bfloat16)
-    for copy in everything:
-        copy.wait_send()
+    for batch in green_copies + wave_copies + [sigma_copies]:
+        for copy in batch:
+            copy.wait_send()
+    for k in order:
+        for chunk in range(CHUNKS):
+            for slot in range(2):
+                polar_copy(k, chunk, slot).wait_send()
+
+    @pl.when(diagonal == 1)
+    def _():
+        for target in range(2):
+            for slot in range(2):
+                more_copy(target, slot).wait_send()
 
 
 def fused_on_device(grid, green_blocks, coulomb, couple_cols, couple_vals):
@@ -391,10 +553,18 @@
     orbitals = green_blocks.shape[-1]
     size = orbitals // grid
     half_type = jnp.bfloat16
-    pieces = pltpu.VMEM((volume, 2, size, size), half_type)
-    whole = pltpu.VMEM((orbitals, orbitals), half_type)
-    block = pltpu.VMEM((size, size), half_type)
+
+    def pieces(*lead):
+        return pltpu.VMEM((*lead, size, size), half_type)
+
+    def wholes(*lead, kind=half_type):
+        return pltpu.VMEM((*lead, orbitals, orbitals), kind)
+
+    def pair(*lead):
+        return [pltpu.SemaphoreType.DMA(lead), pltpu.SemaphoreType.DMA(lead)]
+
     wide = pltpu.VMEM((size, size), jnp.float32)
+    classes = volume // 2
     result = pl.pallas_call(
         functools.partial(
             fused_kernel, volume, slabs, grid,
@@ -404,12 +574,13 @@
         in_specs=[pl.BlockSpec(memory_space=pltpu.HBM)] * 4,
         out_specs=pl.BlockSpec(memory_space=pltpu.VMEM),
         scratch_shapes=[
-            whole, whole, pltpu.VMEM(couple_cols.shape[:0:-1], jnp.int32), pltpu.VMEM(couple_vals.shape[:0:-1], half_type),
-            pieces, pltpu.VMEM((volume, 2, size, size), jnp.float32), pieces, pieces,
-            whole, whole, whole, pieces, pieces, pieces,
-            block, block, block, wide, wide, wide, pltpu.VMEM((orbitals, orbitals), jnp.float32),
-            pltpu.SemaphoreType.DMA((4, volume, 2)), pltpu.SemaphoreType.DMA((4, volume, 2)),
-            pltpu.SemaphoreType.DMA((2,)), pltpu.SemaphoreType.DMA((2,)), pltpu.SemaphoreType.DMA((4,)),
+            wholes(), wholes(), pltpu.VMEM(couple_cols.shape[:0:-1], jnp.int32), pltpu.VMEM(couple_vals.shape[:0:-1], half_type),
+            pieces(volume), pieces(volume, 2), pieces(volume, 2), pieces(volume), pieces(classes, 2), pieces(2),
+            wholes(2), wholes(2), wholes(2, kind=jnp.float32), wholes(2),
+            pieces(classes, 2, 2), pieces(volume, 2), wholes(),
+            pieces(), pieces(), pieces(), wide, wide, wide,
+            *pair(volume, CHUNKS, 2), *pair(volume, CHUNKS, 2), *pair(2, 2), *pair(classes, 2), *pair(volume, 2),
+            *pair(2), pltpu.SemaphoreType.DMA((4,)),
         ],
         compiler_params=pltpu.CompilerParams(
             collective_id=0, has_side_effects=True, vmem_limit_bytes=67043328
@@ -427,7 +598,7 @@
 def on_any(grid, green_blocks, coulomb, couple_cols, couple_vals):
     orbitals = green_blocks.shape[-1]
     fits = (
-        grid > 0
+        grid > 2
         and green_blocks.shape[:2] == (1, 1)
         and orbitals % (128 * max(grid, 1)) == 0
         and couple_cols.shape[1] * grid == orbitals

time: 60.7 us -> 56.3 us (0.928)
  Pallas kernels: 58 us -> 54.2 us
    pallas_call x1, Pallas kernels: 58 us -> 54.2 us  [fused_on_device(): pl.pallas_call(functools.partial(fused_kernel, volume, slabs, grid, 0.5 /...]
where the time goes in v1:
time: 56.3 us; the launch traced here: 56.1 us
  Pallas kernels  54.2 us (96%)
  local copies, waits for them, and re-layouts  1.87 us (3%)
    pallas_call x1, Pallas kernels, fused_on_device(): pl.pallas_call(functools.partial(fused_kernel, volume, slabs, grid, 0.5 /...  54.2 us
    unnamed x1, local copies, waits for them, and re-layouts  1.87 us

profile of v1, /device:TPU:0, one launch (start us, length us, event | category | flops | bytes accessed | tf_op | source)
XLA Modules:
  0.0 56.1 jit_solution(12825949610723846270)
XLA Ops:
  0.0 54.2 %shard_map.46 = bf16[512,512]{1,0:T(8,128)(2,1)} custom-call(bf16[512,512]{1,0:T(8,128)(2,1)} %bitcast.10, bf16[512,512]{1,0:T(8,128)(2,1)} %bitcast.11, s32[8,128]{1,0:T(8,128)} %bitcast.12, bf16[8,128]{1,0:T(8,128)(2,1)} %bitcast.13), custom_call_target="tpu_custom_call" | custom-call | tf_op jit(solution)/shard_map/pallas_call | solution.py:568
  54.2 1.9 %copy.6 = bf16[1,1,512,512]{3,2,1,0:T(8,128)(2,1)} copy(bf16[1,1,512,512]{3,2,1,0:T(8,128)(2,1)} %bitcast.9) | data formatting | bytes 1048576

commit v2 on v1

--- a/solution.py
+++ b/solution.py
@@ -169,6 +169,7 @@
 
 
 CHUNKS = 2
+SUBS = 2
 
 
 def fused_kernel(
@@ -248,12 +249,15 @@
 
     pl.semaphore_wait(barrier, volume - 1 + has_prev + has_next)
 
+    def took(shape, sem):
+        pltpu.make_async_copy(shape, shape, sem).wait()
+
+    others = pl.ds(0, volume - 1)
+
     def span(chunk):
         return pl.ds(chunk * chunk_rows, chunk_rows)
 
-    green_copies = []
     for chunk in range(CHUNKS):
-        batch = []
         for slot in range(2):
             for k in order:
                 peer = peer_of(k)
@@ -262,13 +266,9 @@
                     source = block_of(green, coords, chunk * chunk_rows, chunk_rows)
                 else:
                     source = stage.at[peer, span(chunk)]
-                copy = remote(
-                    source, landed.at[me, slot, span(chunk)],
-                    g_send.at[k, chunk, slot], g_recv.at[k, chunk, slot], peer,
-                )
-                copy.start()
-                batch.append(copy)
-        green_copies.append(batch)
+                remote(
+                    source, landed.at[me, slot, span(chunk)], g_send.at[0], g_recv.at[k, chunk], peer
+                ).start()
     landed[me, 0] = block_of(green, own_blocks[0])[...]
     landed[me, 1] = stage[me]
 
@@ -331,7 +331,7 @@
         return remote(
             polar_out.at[lax.rem(peer, classes), slot, span(chunk)],
             block_of(matrix.at[index], coords, chunk * chunk_rows, chunk_rows),
-            p_send.at[k, chunk, slot], p_recv.at[k, chunk, slot], peer,
+            p_send.at[0], p_recv.at[k], peer,
         )
 
     def send_polar(chunk):
@@ -343,17 +343,17 @@
         return remote(
             polar_more.at[slot],
             block_of(matrix.at[1], own_blocks[slot]),
-            m_send.at[target, slot], m_recv.at[lax.rem(me, paired), slot], target * classes,
+            m_send.at[0], m_recv.at[0], target * classes,
         )
 
-    def arrived(copies):
-        for copy in copies:
-            copy.wait_recv()
+    def green_arrived(k, chunk):
+        took(landed.at[from_of(k), :, span(chunk)], g_recv.at[k, chunk])
 
     @pl.when(diagonal == 0)
     def _():
         for chunk in range(CHUNKS):
-            arrived(green_copies[chunk])
+            for k in order:
+                green_arrived(k, chunk)
 
             def correlate(step, carry):
                 rows = rows_of(step)
@@ -377,10 +377,9 @@
                 mirror[e, slot] = flipped(landed[e, slot])
 
         flip_both(me)
-        for n, k in enumerate(order):
-            for batch in green_copies:
-                for slot in range(2):
-                    batch[slot * len(order) + n].wait_recv()
+        for k in order:
+            for chunk in range(CHUNKS):
+                green_arrived(k, chunk)
             flip_both(from_of(k))
 
         for slot in range(2):
@@ -437,19 +436,12 @@
 
     complete(me)
     for k in order:
-        for chunk in range(CHUNKS):
-            for slot in range(2):
-                polar_copy(k, chunk, slot).wait_recv()
+        took(polar_out.at[0], p_recv.at[k])
         complete(from_of(k))
 
     @pl.when(my_class == 0)
     def _():
-        for unit in range(paired, volume):
-            for slot in range(2):
-                remote(
-                    polar_more.at[slot], block_of(matrix.at[1], unit_blocks(unit, grid)[slot]),
-                    m_send.at[0, slot], m_recv.at[unit - paired, slot], first_mate,
-                ).wait_recv()
+        took(polar_out.at[pl.ds(0, volume - paired)], m_recv.at[0])
 
     for index in range(2):
         inner[index] = plain_dot(coulomb[...], matrix[index]).astype(jnp.bfloat16)
@@ -461,26 +453,37 @@
         third = plain_dot(inner[index], matrix[index])
         screened[index] = (coulomb[...].astype(jnp.float32) + second[index] + third).astype(jnp.bfloat16)
 
-    wave_copies = []
-    for half in range(2):
-        batch = []
+    parts = [(half, sub) for half in range(2) for sub in range(SUBS)]
+    sub_rows = size // SUBS
+    for half, sub in parts:
         for t in range(1, classes):
             mate = first_mate + lax.rem(my_class + t, classes)
-            rows, width = region(unit_blocks(mate, grid)[half])
-            copy = remote(
-                screened.at[:, rows, width], screen_in.at[my_class, half],
-                w_send.at[t, half], w_recv.at[t, half], mate,
-            )
-            copy.start()
-            batch.append(copy)
-        wave_copies.append(batch)
+            rows, width = region(unit_blocks(mate, grid)[half], sub * sub_rows, sub_rows)
+            remote(
+                screened.at[:, rows, width],
+                screen_in.at[my_class, half, :, pl.ds(sub * sub_rows, sub_rows)],
+                w_send.at[0], w_recv.at[half, sub], mate,
+            ).start()
     for half in range(2):
         rows, width = region(own_blocks[half])
         screen_in[my_class, half] = screened[:, rows, width]
 
-    sigma_copies = []
-    for half in range(2):
-        arrived(wave_copies[half])
+    def sigma_copy(half, sub, target):
+        return remote(
+            sigma_out.at[target, half, pl.ds(sub * sub_rows, sub_rows)],
+            block_of(sigma, own_blocks[half], sub * sub_rows, sub_rows),
+            s_send.at[0], s_recv.at[0], target,
+        )
+
+    def for_others(act):
+        for other in range(volume):
+            pl.when(me != other)(functools.partial(act, other))
+
+    for half, sub in parts:
+        took(
+            screen_in.at[pl.ds(0, classes - 1), half, :, pl.ds(sub * sub_rows, sub_rows)],
+            w_recv.at[half, sub],
+        )
 
         def convolve(step, carry, half=half):
             rows = rows_of(step)
@@ -499,15 +502,9 @@
                 sigma_out[e, half, rows, :] = (acc * scale_sigma).astype(jnp.bfloat16)
             return carry
 
-        lax.fori_loop(0, size // rows_at_once, convolve, 0)
-        for k in order:
-            peer = peer_of(k)
-            copy = remote(
-                sigma_out.at[peer, half], block_of(sigma, own_blocks[half]),
-                s_send.at[k, half], s_recv.at[k, half], peer,
-            )
-            copy.start()
-            sigma_copies.append(copy)
+        lax.fori_loop(sub * sub_rows // rows_at_once, (sub + 1) * sub_rows // rows_at_once, convolve, 0)
+        for_others(lambda target: sigma_copy(half, sub, target).start())
+    for half in range(2):
         block_of(sigma, own_blocks[half])[...] = sigma_out[me, half]
 
     @pl.when(slab < slabs - 1)
@@ -516,7 +513,7 @@
         near_next = plain_dot(coupling[...], next_corner[...]).astype(jnp.bfloat16)
         right_in[...] = plain_dot(near_next, turned[...]) * inv_root
 
-    arrived(sigma_copies)
+    took(landed.at[others], s_recv.at[0])
 
     @pl.when(slab < slabs - 1)
     def _():
@@ -532,19 +529,14 @@
     inner[0] = plain_dot(green[...], sigma[...]).astype(jnp.bfloat16)
     updated = green[...].astype(jnp.float32) + plain_dot(inner[0], green[...]) * inv_root
     out[...] = updated.astype(jnp.bfloat16)
-    for batch in green_copies + wave_copies + [sigma_copies]:
-        for copy in batch:
-            copy.wait_send()
-    for k in order:
-        for chunk in range(CHUNKS):
-            for slot in range(2):
-                polar_copy(k, chunk, slot).wait_send()
+    took(landed.at[others], g_send.at[0])
+    took(landed.at[others], p_send.at[0])
+    took(screen_in.at[pl.ds(0, classes - 1)], w_send.at[0])
+    took(landed.at[others], s_send.at[0])
 
     @pl.when(diagonal == 1)
     def _():
-        for target in range(2):
-            for slot in range(2):
-                more_copy(target, slot).wait_send()
+        took(polar_out.at[pl.ds(0, 2)], m_send.at[0])
 
 
 def fused_on_device(grid, green_blocks, coulomb, couple_cols, couple_vals):
@@ -560,8 +552,8 @@
     def wholes(*lead, kind=half_type):
         return pltpu.VMEM((*lead, orbitals, orbitals), kind)
 
-    def pair(*lead):
-        return [pltpu.SemaphoreType.DMA(lead), pltpu.SemaphoreType.DMA(lead)]
+    def pair(sends, recvs):
+        return [pltpu.SemaphoreType.DMA(sends), pltpu.SemaphoreType.DMA(recvs)]
 
     wide = pltpu.VMEM((size, size), jnp.float32)
     classes = volume // 2
@@ -579,8 +571,8 @@
             wholes(2), wholes(2), wholes(2, kind=jnp.float32), wholes(2),
             pieces(classes, 2, 2), pieces(volume, 2), wholes(),
             pieces(), pieces(), pieces(), wide, wide, wide,
-            *pair(volume, CHUNKS, 2), *pair(volume, CHUNKS, 2), *pair(2, 2), *pair(classes, 2), *pair(volume, 2),
-            *pair(2), pltpu.SemaphoreType.DMA((4,)),
+            *pair((1,), (volume, CHUNKS)), *pair((1,), (volume,)), *pair((1,), (1,)),
+            *pair((1,), (2, SUBS)), *pair((1,), (1,)), *pair((2,), (2,)), pltpu.SemaphoreType.DMA((4,)),
         ],
         compiler_params=pltpu.CompilerParams(
             collective_id=0, has_side_effects=True, vmem_limit_bytes=67043328

time: 56.3 us -> 53.5 us (0.950)
  Pallas kernels: 54.2 us -> 51.5 us
    pallas_call x1, Pallas kernels: 54.2 us -> 51.5 us  [fused_on_device(): pl.pallas_call(functools.partial(fused_kernel, volume, slabs, grid, 0.5 /...]
where the time goes in v2:
time: 53.5 us; the launch traced here: 53.4 us
  Pallas kernels  51.5 us (96%)
  local copies, waits for them, and re-layouts  1.87 us (3%)
    pallas_call x1, Pallas kernels, fused_on_device(): pl.pallas_call(functools.partial(fused_kernel, volume, slabs, grid, 0.5 /...  51.5 us
    unnamed x1, local copies, waits for them, and re-layouts  1.87 us

profile of v2, /device:TPU:0, one launch (start us, length us, event | category | flops | bytes accessed | tf_op | source)
XLA Modules:
  0.0 53.4 jit_solution(8488972048172658678)
XLA Ops:
  0.0 51.5 %shard_map.46 = bf16[512,512]{1,0:T(8,128)(2,1)} custom-call(bf16[512,512]{1,0:T(8,128)(2,1)} %bitcast.10, bf16[512,512]{1,0:T(8,128)(2,1)} %bitcast.11, s32[8,128]{1,0:T(8,128)} %bitcast.12, bf16[8,128]{1,0:T(8,128)(2,1)} %bitcast.13), custom_call_target="tpu_custom_call" | custom-call | tf_op jit(solution)/shard_map/pallas_call | solution.py:560
  51.5 1.9 %copy.6 = bf16[1,1,512,512]{3,2,1,0:T(8,128)(2,1)} copy(bf16[1,1,512,512]{3,2,1,0:T(8,128)(2,1)} %bitcast.9) | data formatting | bytes 1048576

commit v3 on v2

--- a/solution.py
+++ b/solution.py
@@ -169,18 +169,20 @@
 
 
 CHUNKS = 2
+GREEN_AHEAD = 2
+POLAR_AHEAD = 2
 SUBS = 2
 
 
 def fused_kernel(
     volume, slabs, grid, scale_polar, scale_sigma, inv_root,
-    green_hbm, coulomb_hbm, cols_hbm, vals_hbm, out,
-    green, coulomb, cols, vals,
+    green_hbm, coulomb_hbm, cols_hbm, vals_hbm, sigma, green,
+    coulomb, cols, vals,
     stage, landed, mirror, second_half, polar_out, polar_more, matrix, inner, second, screened,
-    screen_in, sigma_out, sigma,
+    screen_in, sigma_out,
     coupling, turned, next_corner, left_out, left_in, right_in,
     g_send, g_recv, p_send, p_recv, m_send, m_recv, w_send, w_recv, s_send, s_recv,
-    slab_send, slab_recv, load_sem,
+    slab_send, slab_recv, load_sem, turn,
 ):
     loads = [
         pltpu.make_async_copy(source, target, load_sem.at[n])
@@ -267,7 +269,7 @@
                 else:
                     source = stage.at[peer, span(chunk)]
                 remote(
-                    source, landed.at[me, slot, span(chunk)], g_send.at[0], g_recv.at[k, chunk], peer
+                    source, landed.at[me, slot, span(chunk)], g_send.at[chunk], g_recv.at[k, chunk], peer
                 ).start()
     landed[me, 0] = block_of(green, own_blocks[0])[...]
     landed[me, 1] = stage[me]
@@ -305,6 +307,14 @@
         left_out[...] = plain_dot(near_prev, coupling[...]) * inv_root
         left_copy.start()
 
+    second_core = lax.rem(slab, 2)
+
+    @pl.when(second_core == 0)
+    def _():
+        for chunk in range(GREEN_AHEAD):
+            took(landed.at[others, :, span(chunk)], g_send.at[chunk])
+        pl.semaphore_signal(turn.at[0], inc=1, device_id=(me, slab + 1), device_id_type=MESH)
+
     loads[1].wait()
     rows_at_once = 16
     steps = chunk_rows // rows_at_once
@@ -331,10 +341,12 @@
         return remote(
             polar_out.at[lax.rem(peer, classes), slot, span(chunk)],
             block_of(matrix.at[index], coords, chunk * chunk_rows, chunk_rows),
-            p_send.at[0], p_recv.at[k], peer,
+            p_send.at[chunk], p_recv.at[k], peer,
         )
 
     def send_polar(chunk):
+        if chunk == 0:
+            pl.semaphore_wait(turn.at[0], 1)
         for slot in range(2):
             for k in order:
                 polar_copy(k, chunk, slot).start()
@@ -412,6 +424,12 @@
     def _():
         for e in range(volume):
             second_half[e] = landed[e, 1]
+
+    @pl.when(second_core == 1)
+    def _():
+        for chunk in range(POLAR_AHEAD):
+            took(landed.at[others, :, span(chunk)], p_send.at[chunk])
+        pl.semaphore_signal(turn.at[0], inc=1, device_id=(me, slab - 1), device_id_type=MESH)
 
     swapped = 1 - lax.rem(my_class + classes - 1, classes) // (classes - 1)
 
@@ -526,17 +544,27 @@
         sigma[:size, :size] = (sigma[:size, :size].astype(jnp.float32) + left_in[...]).astype(jnp.bfloat16)
         corner_copy.wait_send()
 
-    inner[0] = plain_dot(green[...], sigma[...]).astype(jnp.bfloat16)
-    updated = green[...].astype(jnp.float32) + plain_dot(inner[0], green[...]) * inv_root
-    out[...] = updated.astype(jnp.bfloat16)
-    took(landed.at[others], g_send.at[0])
-    took(landed.at[others], p_send.at[0])
+    for chunk in range(CHUNKS):
+        @pl.when(second_core + (chunk >= GREEN_AHEAD) > 0)
+        def _():
+            took(landed.at[others, :, span(chunk)], g_send.at[chunk])
+
+        @pl.when(1 - second_core + (chunk >= POLAR_AHEAD) > 0)
+        def _():
+            took(landed.at[others, :, span(chunk)], p_send.at[chunk])
+
     took(screen_in.at[pl.ds(0, classes - 1)], w_send.at[0])
     took(landed.at[others], s_send.at[0])
 
     @pl.when(diagonal == 1)
     def _():
         took(polar_out.at[pl.ds(0, 2)], m_send.at[0])
+
+
+def dress_kernel(inv_root, total, green, out):
+    dressed = plain_dot(green[...], total[...]).astype(jnp.bfloat16)
+    updated = green[...].astype(jnp.float32) + plain_dot(dressed, green[...]) * inv_root
+    out[...] = updated.astype(jnp.bfloat16)
 
 
 def fused_on_device(grid, green_blocks, coulomb, couple_cols, couple_vals):
@@ -557,27 +585,40 @@
 
     wide = pltpu.VMEM((size, size), jnp.float32)
     classes = volume // 2
-    result = pl.pallas_call(
+    inv_root = 1.0 / math.sqrt(orbitals)
+    in_vmem = pl.BlockSpec(memory_space=pltpu.VMEM)
+    total, green = pl.pallas_call(
         functools.partial(
             fused_kernel, volume, slabs, grid,
-            0.5 / math.sqrt(orbitals * volume), 0.2 / math.sqrt(volume), 1.0 / math.sqrt(orbitals),
+            0.5 / math.sqrt(orbitals * volume), 0.2 / math.sqrt(volume), inv_root,
         ),
-        out_shape=jax.ShapeDtypeStruct((orbitals, orbitals), half_type),
+        out_shape=[jax.ShapeDtypeStruct((orbitals, orbitals), half_type)] * 2,
         in_specs=[pl.BlockSpec(memory_space=pltpu.HBM)] * 4,
-        out_specs=pl.BlockSpec(memory_space=pltpu.VMEM),
+        out_specs=[in_vmem] * 2,
         scratch_shapes=[
-            wholes(), wholes(), pltpu.VMEM(couple_cols.shape[:0:-1], jnp.int32), pltpu.VMEM(couple_vals.shape[:0:-1], half_type),
+            wholes(), pltpu.VMEM(couple_cols.shape[:0:-1], jnp.int32), pltpu.VMEM(couple_vals.shape[:0:-1], half_type),
             pieces(volume), pieces(volume, 2), pieces(volume, 2), pieces(volume), pieces(classes, 2), pieces(2),
             wholes(2), wholes(2), wholes(2, kind=jnp.float32), wholes(2),
-            pieces(classes, 2, 2), pieces(volume, 2), wholes(),
+            pieces(classes, 2, 2), pieces(volume, 2),
             pieces(), pieces(), pieces(), wide, wide, wide,
-            *pair((1,), (volume, CHUNKS)), *pair((1,), (volume,)), *pair((1,), (1,)),
+            *pair((CHUNKS,), (volume, CHUNKS)), *pair((CHUNKS,), (volume,)), *pair((1,), (1,)),
             *pair((1,), (2, SUBS)), *pair((1,), (1,)), *pair((2,), (2,)), pltpu.SemaphoreType.DMA((4,)),
+            pltpu.SemaphoreType.REGULAR((2,)),
         ],
         compiler_params=pltpu.CompilerParams(
-            collective_id=0, has_side_effects=True, vmem_limit_bytes=67043328
+            collective_id=0, has_side_effects=True, vmem_limit_bytes=32 << 20
         ),
-    )(green_blocks[0, 0], coulomb[0], couple_cols[0].T, couple_vals[0].T)
+    )(*(
+        pltpu.with_memory_space_constraint(array, pltpu.HBM)
+        for array in (green_blocks[0, 0], coulomb[0], couple_cols[0].T, couple_vals[0].T)
+    ))
+    result = pl.pallas_call(
+        functools.partial(dress_kernel, inv_root),
+        out_shape=jax.ShapeDtypeStruct((orbitals, orbitals), half_type),
+        in_specs=[in_vmem] * 2,
+        out_specs=in_vmem,
+        compiler_params=pltpu.CompilerParams(vmem_limit_bytes=16 << 20),
+    )(total, green)
     return result[None, None]
 
 
@@ -594,7 +635,7 @@
         and green_blocks.shape[:2] == (1, 1)
         and orbitals % (128 * max(grid, 1)) == 0
         and couple_cols.shape[1] * grid == orbitals
-        and lax.axis_size("slab") > 1
+        and lax.axis_size("slab") % 2 == 0
     )
     if fits:
         return fused_on_device(grid, green_blocks, coulomb, couple_cols, couple_vals)

time: 53.5 us -> 49.8 us (0.931)
  Pallas kernels: 51.5 us -> 49.6 us
  local copies, waits for them, and re-layouts: 1.87 us -> 0 us
    pallas_call x1, Pallas kernels: 51.5 us -> 48.1 us  [fused_on_device(): pl.pallas_call(functools.partial(fused_kernel, volume, slabs, grid, 0.5 /...]
    unnamed x1 -> x0, local copies, waits for them, and re-layouts: 1.87 us -> none
    pallas_call x0 -> x1, Pallas kernels: none -> 1.51 us  [fused_on_device(): pl.pallas_call(functools.partial(dress_kernel, inv_root), out_shape=jax.S...]
where the time goes in v3:
time: 49.8 us; the launch traced here: 49.6 us
  Pallas kernels  49.6 us (100%)
    pallas_call x1, Pallas kernels, fused_on_device(): pl.pallas_call(functools.partial(fused_kernel, volume, slabs, grid, 0.5 /...  48.1 us
    pallas_call x1, Pallas kernels, fused_on_device(): pl.pallas_call(functools.partial(dress_kernel, inv_root), out_shape=jax.S...  1.51 us

profile of v3, /device:TPU:0, one launch (start us, length us, event | category | flops | bytes accessed | tf_op | source)
XLA Modules:
  0.0 49.6 jit_solution(1940634829484128220)
XLA Ops:
  0.0 48.1 %shard_map.46 = (bf16[512,512]{1,0:T(8,128)(2,1)S(1)}, bf16[512,512]{1,0:T(8,128)(2,1)S(1)}) custom-call(bf16[512,512]{1,0:T(8,128)(2,1)} %bitcast.9, bf16[512,512]{1,0:T(8,128)(2,1)} %bitcast.10, s32[8,128]{1,0:T(8,128)} %bitcast.11, bf16[8,128]{1,0:T(8,128)(2,1)} %bitcast.12), custom_call_target="tpu_custom_call" | custom-call | tf_op jit(solution)/shard_map/pallas_call | solution.py:590
  48.1 1.5 %shard_map.47 = bf16[512,512]{1,0:T(8,128)(2,1)} custom-call(bf16[512,512]{1,0:T(8,128)(2,1)S(1)} %get-tuple-element.7.total, bf16[512,512]{1,0:T(8,128)(2,1)S(1)} %get-tuple-element.8.green), custom_call_target="tpu_custom_call" | custom-call | tf_op jit(solution)/shard_map/pallas_call | solution.py:615

commit v4 on v3

--- a/solution.py
+++ b/solution.py
@@ -168,9 +168,9 @@
     return ((row0, col0), (row1, col1))
 
 
-CHUNKS = 2
-GREEN_AHEAD = 2
-POLAR_AHEAD = 2
+CHUNKS = 1
+GREEN_AHEAD = 1
+POLAR_AHEAD = 1
 SUBS = 2
 
 
@@ -182,7 +182,7 @@
     screen_in, sigma_out,
     coupling, turned, next_corner, left_out, left_in, right_in,
     g_send, g_recv, p_send, p_recv, m_send, m_recv, w_send, w_recv, s_send, s_recv,
-    slab_send, slab_recv, load_sem, turn,
+    slab_send, slab_recv, load_sem, turn, ready,
 ):
     loads = [
         pltpu.make_async_copy(source, target, load_sem.at[n])
@@ -201,10 +201,19 @@
     order = sorted(range(1, volume), key=lambda k: (-min(k, volume - k), k))
     has_prev = 1 - (slabs - 1 - slab + 0) // (slabs - 1)
     has_next = 1 - slab // (slabs - 1)
-    diagonal = me // paired
+    planes = 4
+    plane = volume // planes
+    level = me // plane
+    inner_level = level * (planes - 1 - level) // (planes - 2)
+
+    def unit_of(device):
+        return lax.rem(device + volume // 2, volume)
+
+    my_unit = unit_of(me)
+    diagonal = my_unit // paired
     my_class = lax.rem(me, classes)
     first_mate = me - my_class
-    own_blocks = unit_blocks(me, grid)
+    own_blocks = unit_blocks(my_unit, grid)
     chunk_rows = size // CHUNKS
 
     def peer_of(k):
@@ -214,8 +223,15 @@
         return lax.rem(me + volume - k, volume)
 
     barrier = pltpu.get_barrier_semaphore()
-    for k in range(1, volume):
-        pl.semaphore_signal(barrier, inc=1, device_id=(peer_of(k), slab), device_id_type=MESH)
+
+    def apart(device):
+        steps = device // plane - level
+        return steps * steps
+
+    for k in order:
+        @pl.when(apart(peer_of(k)) <= 1)
+        def _():
+            pl.semaphore_signal(barrier, inc=1, device_id=(peer_of(k), slab), device_id_type=MESH)
 
     @pl.when(slab > 0)
     def _():
@@ -249,7 +265,16 @@
         block = green[coords[0] * size:(coords[0] + 1) * size, coords[1] * size:(coords[1] + 1) * size]
         stage[unit] = block if unit >= paired else flipped(block)
 
-    pl.semaphore_wait(barrier, volume - 1 + has_prev + has_next)
+    pl.semaphore_wait(barrier, (2 + inner_level) * plane - 1 + has_prev + has_next)
+
+    def tell(step, which):
+        pl.semaphore_signal(ready.at[which], inc=1, device_id=(me + step * plane, slab), device_id_type=MESH)
+
+    @pl.when(inner_level > 0)
+    def _():
+        tell(1, 0)
+        tell(-1, 0)
+
 
     def took(shape, sem):
         pltpu.make_async_copy(shape, shape, sem).wait()
@@ -259,20 +284,44 @@
     def span(chunk):
         return pl.ds(chunk * chunk_rows, chunk_rows)
 
-    for chunk in range(CHUNKS):
-        for slot in range(2):
-            for k in order:
-                peer = peer_of(k)
-                coords = unit_blocks(peer, grid)[0]
+    def send_green(k):
+        peer = peer_of(k)
+        unit = unit_of(peer)
+        for chunk in range(CHUNKS):
+            for slot in range(2):
                 if slot == 0:
-                    source = block_of(green, coords, chunk * chunk_rows, chunk_rows)
+                    source = block_of(green, unit_blocks(unit, grid)[0], chunk * chunk_rows, chunk_rows)
                 else:
-                    source = stage.at[peer, span(chunk)]
+                    source = stage.at[unit, span(chunk)]
                 remote(
                     source, landed.at[me, slot, span(chunk)], g_send.at[chunk], g_recv.at[k, chunk], peer
                 ).start()
+
+    def send_tier(low, high):
+        for k in order:
+            distance = apart(peer_of(k))
+            pl.when(jnp.logical_and(distance >= low, distance <= high))(functools.partial(send_green, k))
+
+    send_tier(0, 1)
+    pl.semaphore_wait(ready.at[0], 1)
+
+    @pl.when(level == 1)
+    def _():
+        tell(-1, 1)
+
+    @pl.when(level == 2)
+    def _():
+        tell(1, 1)
+
+    send_tier(4, 4)
+
+    @pl.when(inner_level == 0)
+    def _():
+        pl.semaphore_wait(ready.at[1], 1)
+        send_tier(9, 9)
+
     landed[me, 0] = block_of(green, own_blocks[0])[...]
-    landed[me, 1] = stage[me]
+    landed[me, 1] = stage[my_unit]
 
     corner_copy = pltpu.make_async_remote_copy(
         src_ref=green.at[pl.ds(0, size), pl.ds(0, size)], dst_ref=next_corner,
@@ -433,7 +482,8 @@
 
     swapped = 1 - lax.rem(my_class + classes - 1, classes) // (classes - 1)
 
-    def complete(unit):
+    def complete(device):
+        unit = unit_of(device)
         coords = unit_blocks(unit, grid)
         off = 1 - unit // paired
 
@@ -476,7 +526,7 @@
     for half, sub in parts:
         for t in range(1, classes):
             mate = first_mate + lax.rem(my_class + t, classes)
-            rows, width = region(unit_blocks(mate, grid)[half], sub * sub_rows, sub_rows)
+            rows, width = region(unit_blocks(unit_of(mate), grid)[half], sub * sub_rows, sub_rows)
             remote(
                 screened.at[:, rows, width],
                 screen_in.at[my_class, half, :, pl.ds(sub * sub_rows, sub_rows)],
@@ -603,7 +653,7 @@
             pieces(), pieces(), pieces(), wide, wide, wide,
             *pair((CHUNKS,), (volume, CHUNKS)), *pair((CHUNKS,), (volume,)), *pair((1,), (1,)),
             *pair((1,), (2, SUBS)), *pair((1,), (1,)), *pair((2,), (2,)), pltpu.SemaphoreType.DMA((4,)),
-            pltpu.SemaphoreType.REGULAR((2,)),
+            pltpu.SemaphoreType.REGULAR((1,)), pltpu.SemaphoreType.REGULAR((2,)),
         ],
         compiler_params=pltpu.CompilerParams(
             collective_id=0, has_side_effects=True, vmem_limit_bytes=32 << 20

time: 49.8 us -> 48.8 us (0.980)
  Pallas kernels: 49.6 us -> 48.7 us
    pallas_call x1, Pallas kernels: 48.1 us -> 47.2 us  [fused_on_device(): pl.pallas_call(functools.partial(fused_kernel, volume, slabs, grid, 0.5 /...]
where the time goes in v4:
time: 48.8 us; the launch traced here: 48.7 us
  Pallas kernels  48.7 us (100%)
    pallas_call x1, Pallas kernels, fused_on_device(): pl.pallas_call(functools.partial(fused_kernel, volume, slabs, grid, 0.5 /...  47.2 us
    pallas_call x1, Pallas kernels, fused_on_device(): pl.pallas_call(functools.partial(dress_kernel, inv_root), out_shape=jax.S...  1.51 us

profile of v4, /device:TPU:0, one launch (start us, length us, event | category | flops | bytes accessed | tf_op | source)
XLA Modules:
  0.0 48.7 jit_solution(3754637670436550255)
XLA Ops:
  0.0 47.2 %shard_map.46 = (bf16[512,512]{1,0:T(8,128)(2,1)S(1)}, bf16[512,512]{1,0:T(8,128)(2,1)S(1)}) custom-call(bf16[512,512]{1,0:T(8,128)(2,1)} %bitcast.9, bf16[512,512]{1,0:T(8,128)(2,1)} %bitcast.10, s32[8,128]{1,0:T(8,128)} %bitcast.11, bf16[8,128]{1,0:T(8,128)(2,1)} %bitcast.12), custom_call_target="tpu_custom_call" | custom-call | tf_op jit(solution)/shard_map/pallas_call | solution.py:640
  47.2 1.5 %shard_map.47 = bf16[512,512]{1,0:T(8,128)(2,1)} custom-call(bf16[512,512]{1,0:T(8,128)(2,1)S(1)} %get-tuple-element.7.total, bf16[512,512]{1,0:T(8,128)(2,1)S(1)} %get-tuple-element.8.green), custom_call_target="tpu_custom_call" | custom-call | tf_op jit(solution)/shard_map/pallas_call | solution.py:665

commit v5 on v4

--- a/solution.py
+++ b/solution.py
@@ -172,6 +172,8 @@
 GREEN_AHEAD = 1
 POLAR_AHEAD = 1
 SUBS = 2
+FIRST = 2
+LATE = 2
 
 
 def fused_kernel(
@@ -201,7 +203,7 @@
     order = sorted(range(1, volume), key=lambda k: (-min(k, volume - k), k))
     has_prev = 1 - (slabs - 1 - slab + 0) // (slabs - 1)
     has_next = 1 - slab // (slabs - 1)
-    planes = 4
+    planes = volume // 2
     plane = volume // planes
     level = me // plane
     inner_level = level * (planes - 1 - level) // (planes - 2)
@@ -228,8 +230,14 @@
         steps = device // plane - level
         return steps * steps
 
+    column = lax.rem(me, plane)
+
+    def tier(device):
+        aside = lax.rem(device, plane) - column
+        return apart(device) * (apart(device) + 1) // 2 + aside * aside
+
     for k in order:
-        @pl.when(apart(peer_of(k)) <= 1)
+        @pl.when(tier(peer_of(k)) <= 1)
         def _():
             pl.semaphore_signal(barrier, inc=1, device_id=(peer_of(k), slab), device_id_type=MESH)
 
@@ -265,16 +273,13 @@
         block = green[coords[0] * size:(coords[0] + 1) * size, coords[1] * size:(coords[1] + 1) * size]
         stage[unit] = block if unit >= paired else flipped(block)
 
-    pl.semaphore_wait(barrier, (2 + inner_level) * plane - 1 + has_prev + has_next)
-
-    def tell(step, which):
-        pl.semaphore_signal(ready.at[which], inc=1, device_id=(me + step * plane, slab), device_id_type=MESH)
-
-    @pl.when(inner_level > 0)
-    def _():
-        tell(1, 0)
-        tell(-1, 0)
-
+    pl.semaphore_wait(barrier, inner_level + plane + has_prev + has_next)
+
+    def tell(device, which):
+        pl.semaphore_signal(ready.at[which], inc=1, device_id=(device, slab), device_id_type=MESH)
+
+    for k in range(1, plane):
+        tell(me - column + lax.rem(column + k, plane), 0)
 
     def took(shape, sem):
         pltpu.make_async_copy(shape, shape, sem).wait()
@@ -298,27 +303,35 @@
                 ).start()
 
     def send_tier(low, high):
-        for k in order:
-            distance = apart(peer_of(k))
+        for k in order[::-1]:
+            distance = tier(peer_of(k))
             pl.when(jnp.logical_and(distance >= low, distance <= high))(functools.partial(send_green, k))
 
     send_tier(0, 1)
-    pl.semaphore_wait(ready.at[0], 1)
+    pl.semaphore_wait(ready.at[0], plane - 1)
+
+    @pl.when(inner_level > 0)
+    def _():
+        tell(me + plane, 1)
+        tell(me - plane, 1)
+
+    send_tier(2, 2)
+    pl.semaphore_wait(ready.at[1], 1)
 
     @pl.when(level == 1)
     def _():
-        tell(-1, 1)
+        tell(me - plane, 2)
 
     @pl.when(level == 2)
     def _():
-        tell(1, 1)
-
-    send_tier(4, 4)
+        tell(me + plane, 2)
+
+    send_tier(10, 11)
 
     @pl.when(inner_level == 0)
     def _():
-        pl.semaphore_wait(ready.at[1], 1)
-        send_tier(9, 9)
+        pl.semaphore_wait(ready.at[2], 1)
+        send_tier(45, 46)
 
     landed[me, 0] = block_of(green, own_blocks[0])[...]
     landed[me, 1] = stage[my_unit]
@@ -517,24 +530,30 @@
         product = plain_dot(inner[index], coulomb[...])
         second[index] = product
         matrix[index] = product.astype(jnp.bfloat16)
-    for index in range(2):
-        third = plain_dot(inner[index], matrix[index])
-        screened[index] = (coulomb[...].astype(jnp.float32) + second[index] + third).astype(jnp.bfloat16)
-
     parts = [(half, sub) for half in range(2) for sub in range(SUBS)]
     sub_rows = size // SUBS
-    for half, sub in parts:
+
+    def wave(index, coords):
+        rows, width = region(coords)
+        third = plain_dot(inner[index, rows, :], matrix[index, :, width])
+        whole = coulomb[rows, width].astype(jnp.float32) + second[index, rows, width] + third
+        return whole.astype(jnp.bfloat16)
+
+    for half in range(2):
         for t in range(1, classes):
-            mate = first_mate + lax.rem(my_class + t, classes)
-            rows, width = region(unit_blocks(unit_of(mate), grid)[half], sub * sub_rows, sub_rows)
-            remote(
-                screened.at[:, rows, width],
-                screen_in.at[my_class, half, :, pl.ds(sub * sub_rows, sub_rows)],
-                w_send.at[0], w_recv.at[half, sub], mate,
-            ).start()
+            coords = unit_blocks(unit_of(first_mate + lax.rem(my_class + t, classes)), grid)[half]
+            for index in range(2):
+                screened[t, half, index] = wave(index, coords)
+        for sub in range(SUBS):
+            for t in range(1, classes):
+                span_now = pl.ds(sub * sub_rows, sub_rows)
+                remote(
+                    screened.at[t, half, :, span_now], screen_in.at[my_class, half, :, span_now],
+                    w_send.at[0], w_recv.at[half, sub], first_mate + lax.rem(my_class + t, classes),
+                ).start()
     for half in range(2):
-        rows, width = region(own_blocks[half])
-        screen_in[my_class, half] = screened[:, rows, width]
+        for index in range(2):
+            screen_in[my_class, half, index] = wave(index, own_blocks[half])
 
     def sigma_copy(half, sub, target):
         return remote(
@@ -547,7 +566,11 @@
         for other in range(volume):
             pl.when(me != other)(functools.partial(act, other))
 
-    for half, sub in parts:
+    def send_sigma(n, targets):
+        for target in targets:
+            pl.when(me != target)(lambda: sigma_copy(*parts[n], target).start())
+
+    for n, (half, sub) in enumerate(parts):
         took(
             screen_in.at[pl.ds(0, classes - 1), half, :, pl.ds(sub * sub_rows, sub_rows)],
             w_recv.at[half, sub],
@@ -571,7 +594,11 @@
             return carry
 
         lax.fori_loop(sub * sub_rows // rows_at_once, (sub + 1) * sub_rows // rows_at_once, convolve, 0)
-        for_others(lambda target: sigma_copy(half, sub, target).start())
+        send_sigma(n, range(FIRST))
+        if n >= LATE:
+            send_sigma(n - LATE, range(FIRST, volume))
+    for n in range(len(parts) - LATE, len(parts)):
+        send_sigma(n, range(FIRST, volume))
     for half in range(2):
         block_of(sigma, own_blocks[half])[...] = sigma_out[me, half]
 
@@ -648,12 +675,12 @@
         scratch_shapes=[
             wholes(), pltpu.VMEM(couple_cols.shape[:0:-1], jnp.int32), pltpu.VMEM(couple_vals.shape[:0:-1], half_type),
             pieces(volume), pieces(volume, 2), pieces(volume, 2), pieces(volume), pieces(classes, 2), pieces(2),
-            wholes(2), wholes(2), wholes(2, kind=jnp.float32), wholes(2),
+            wholes(2), wholes(2), wholes(2, kind=jnp.float32), pieces(classes, 2, 2),
             pieces(classes, 2, 2), pieces(volume, 2),
             pieces(), pieces(), pieces(), wide, wide, wide,
             *pair((CHUNKS,), (volume, CHUNKS)), *pair((CHUNKS,), (volume,)), *pair((1,), (1,)),
             *pair((1,), (2, SUBS)), *pair((1,), (1,)), *pair((2,), (2,)), pltpu.SemaphoreType.DMA((4,)),
-            pltpu.SemaphoreType.REGULAR((1,)), pltpu.SemaphoreType.REGULAR((2,)),
+            pltpu.SemaphoreType.REGULAR((1,)), pltpu.SemaphoreType.REGULAR((3,)),
         ],
         compiler_params=pltpu.CompilerParams(
             collective_id=0, has_side_effects=True, vmem_limit_bytes=32 << 20
@@ -682,6 +709,7 @@
     orbitals = green_blocks.shape[-1]
     fits = (
         grid > 2
+        and grid * 2 == lax.axis_size("energy")
         and green_blocks.shape[:2] == (1, 1)
         and orbitals % (128 * max(grid, 1)) == 0
         and couple_cols.shape[1] * grid == orbitals

time: 48.8 us -> 48.1 us (0.986)
  Pallas kernels: 48.7 us -> 47.7 us
    pallas_call x1, Pallas kernels: 47.2 us -> 46.2 us  [fused_on_device(): pl.pallas_call(functools.partial(fused_kernel, volume, slabs, grid, 0.5 /...]
where the time goes in v5:
time: 48.1 us; the launch traced here: 47.7 us
  Pallas kernels  47.7 us (99%)
    pallas_call x1, Pallas kernels, fused_on_device(): pl.pallas_call(functools.partial(fused_kernel, volume, slabs, grid, 0.5 /...  46.2 us
    pallas_call x1, Pallas kernels, fused_on_device(): pl.pallas_call(functools.partial(dress_kernel, inv_root), out_shape=jax.S...  1.51 us

profile of v5, /device:TPU:0, one launch (start us, length us, event | category | flops | bytes accessed | tf_op | source)
XLA Modules:
  0.0 47.7 jit_solution(4838414251598453127)
XLA Ops:
  0.0 46.2 %shard_map.46 = (bf16[512,512]{1,0:T(8,128)(2,1)S(1)}, bf16[512,512]{1,0:T(8,128)(2,1)S(1)}) custom-call(bf16[512,512]{1,0:T(8,128)(2,1)} %bitcast.9, bf16[512,512]{1,0:T(8,128)(2,1)} %bitcast.10, s32[8,128]{1,0:T(8,128)} %bitcast.11, bf16[8,128]{1,0:T(8,128)(2,1)} %bitcast.12), custom_call_target="tpu_custom_call" | custom-call | tf_op jit(solution)/shard_map/pallas_call | solution.py:667
  46.2 1.5 %shard_map.47 = bf16[512,512]{1,0:T(8,128)(2,1)} custom-call(bf16[512,512]{1,0:T(8,128)(2,1)S(1)} %get-tuple-element.7.total, bf16[512,512]{1,0:T(8,128)(2,1)S(1)} %get-tuple-element.8.green), custom_call_target="tpu_custom_call" | custom-call | tf_op jit(solution)/shard_map/pallas_call | solution.py:692

commit v6 on v5

--- a/solution.py
+++ b/solution.py
@@ -169,11 +169,7 @@
 
 
 CHUNKS = 1
-GREEN_AHEAD = 1
-POLAR_AHEAD = 1
 SUBS = 2
-FIRST = 2
-LATE = 2
 
 
 def fused_kernel(
@@ -369,13 +365,14 @@
         left_out[...] = plain_dot(near_prev, coupling[...]) * inv_root
         left_copy.start()
 
-    second_core = lax.rem(slab, 2)
+    second_core = 1 - lax.rem(slab, 2)
+    partner = slab - 1 + 2 * second_core
 
     @pl.when(second_core == 0)
     def _():
-        for chunk in range(GREEN_AHEAD):
+        for chunk in range(CHUNKS):
             took(landed.at[others, :, span(chunk)], g_send.at[chunk])
-        pl.semaphore_signal(turn.at[0], inc=1, device_id=(me, slab + 1), device_id_type=MESH)
+        pl.semaphore_signal(turn.at[0], inc=1, device_id=(me, partner), device_id_type=MESH)
 
     loads[1].wait()
     rows_at_once = 16
@@ -489,9 +486,9 @@
 
     @pl.when(second_core == 1)
     def _():
-        for chunk in range(POLAR_AHEAD):
+        for chunk in range(CHUNKS):
             took(landed.at[others, :, span(chunk)], p_send.at[chunk])
-        pl.semaphore_signal(turn.at[0], inc=1, device_id=(me, slab - 1), device_id_type=MESH)
+        pl.semaphore_signal(turn.at[0], inc=1, device_id=(me, partner), device_id_type=MESH)
 
     swapped = 1 - lax.rem(my_class + classes - 1, classes) // (classes - 1)
 
@@ -567,8 +564,10 @@
             pl.when(me != other)(functools.partial(act, other))
 
     def send_sigma(n, targets):
-        for target in targets:
-            pl.when(me != target)(lambda: sigma_copy(*parts[n], target).start())
+        for target in range(volume):
+            crosses = target // classes != me // classes
+            chosen = crosses if targets else jnp.logical_and(me != target, jnp.logical_not(crosses))
+            pl.when(chosen)(lambda: sigma_copy(*parts[n], target).start())
 
     for n, (half, sub) in enumerate(parts):
         took(
@@ -594,11 +593,8 @@
             return carry
 
         lax.fori_loop(sub * sub_rows // rows_at_once, (sub + 1) * sub_rows // rows_at_once, convolve, 0)
-        send_sigma(n, range(FIRST))
-        if n >= LATE:
-            send_sigma(n - LATE, range(FIRST, volume))
-    for n in range(len(parts) - LATE, len(parts)):
-        send_sigma(n, range(FIRST, volume))
+        send_sigma(n, True)
+        send_sigma(n, False)
     for half in range(2):
         block_of(sigma, own_blocks[half])[...] = sigma_out[me, half]
 
@@ -622,11 +618,11 @@
         corner_copy.wait_send()
 
     for chunk in range(CHUNKS):
-        @pl.when(second_core + (chunk >= GREEN_AHEAD) > 0)
+        @pl.when(second_core > 0)
         def _():
             took(landed.at[others, :, span(chunk)], g_send.at[chunk])
 
-        @pl.when(1 - second_core + (chunk >= POLAR_AHEAD) > 0)
+        @pl.when(second_core == 0)
         def _():
             took(landed.at[others, :, span(chunk)], p_send.at[chunk])
 

time: 48.1 us -> 47.8 us (level)
  the two profiles are of different devices: /device:TPU:0 before, /device:TPU:1 now
where the time goes in v6:
time: 47.8 us; the launch traced here: 47.7 us
  Pallas kernels  47.7 us (100%)
    pallas_call x1, Pallas kernels, fused_on_device(): pl.pallas_call(functools.partial(fused_kernel, volume, slabs, grid, 0.5 /...  46.2 us
    pallas_call x1, Pallas kernels, fused_on_device(): pl.pallas_call(functools.partial(dress_kernel, inv_root), out_shape=jax.S...  1.51 us

profile of v6, /device:TPU:1, one launch (start us, length us, event | category | flops | bytes accessed | tf_op | source)
XLA Modules:
  0.0 47.7 jit_solution(7987644645917033874)
XLA Ops:
  0.0 46.2 %shard_map.46 = (bf16[512,512]{1,0:T(8,128)(2,1)S(1)}, bf16[512,512]{1,0:T(8,128)(2,1)S(1)}) custom-call(bf16[512,512]{1,0:T(8,128)(2,1)} %bitcast.9, bf16[512,512]{1,0:T(8,128)(2,1)} %bitcast.10, s32[8,128]{1,0:T(8,128)} %bitcast.11, bf16[8,128]{1,0:T(8,128)(2,1)} %bitcast.12), custom_call_target="tpu_custom_call" | custom-call | tf_op jit(solution)/shard_map/pallas_call | solution.py:663
  46.2 1.5 %shard_map.47 = bf16[512,512]{1,0:T(8,128)(2,1)} custom-call(bf16[512,512]{1,0:T(8,128)(2,1)S(1)} %get-tuple-element.7.total, bf16[512,512]{1,0:T(8,128)(2,1)S(1)} %get-tuple-element.8.green), custom_call_target="tpu_custom_call" | custom-call | tf_op jit(solution)/shard_map/pallas_call | solution.py:688

commit v7 on v6

--- a/solution.py
+++ b/solution.py
@@ -246,7 +246,7 @@
         pl.semaphore_signal(barrier, inc=1, device_id=(me, slab + 1), device_id_type=MESH)
 
     def flipped(block):
-        return block.astype(jnp.float32).T.astype(jnp.bfloat16)
+        return block.T
 
     def region(coords, start=0, rows=None):
         rows = size if rows is None else rows

time: 47.8 us -> 47.5 us (level)
  no operation moved by 1% of the time
where the time goes in v7:
time: 47.5 us; the launch traced here: 47.3 us
  Pallas kernels  47.3 us (100%)
    pallas_call x1, Pallas kernels, fused_on_device(): pl.pallas_call(functools.partial(fused_kernel, volume, slabs, grid, 0.5 /...  45.8 us
    pallas_call x1, Pallas kernels, fused_on_device(): pl.pallas_call(functools.partial(dress_kernel, inv_root), out_shape=jax.S...  1.51 us

profile of v7, /device:TPU:1, one launch (start us, length us, event | category | flops | bytes accessed | tf_op | source)
XLA Modules:
  0.0 47.3 jit_solution(2595466182619934200)
XLA Ops:
  0.0 45.8 %shard_map.46 = (bf16[512,512]{1,0:T(8,128)(2,1)S(1)}, bf16[512,512]{1,0:T(8,128)(2,1)S(1)}) custom-call(bf16[512,512]{1,0:T(8,128)(2,1)} %bitcast.9, bf16[512,512]{1,0:T(8,128)(2,1)} %bitcast.10, s32[8,128]{1,0:T(8,128)} %bitcast.11, bf16[8,128]{1,0:T(8,128)(2,1)} %bitcast.12), custom_call_target="tpu_custom_call" | custom-call | tf_op jit(solution)/shard_map/pallas_call | solution.py:663
  45.8 1.5 %shard_map.47 = bf16[512,512]{1,0:T(8,128)(2,1)} custom-call(bf16[512,512]{1,0:T(8,128)(2,1)S(1)} %get-tuple-element.7.total, bf16[512,512]{1,0:T(8,128)(2,1)S(1)} %get-tuple-element.8.green), custom_call_target="tpu_custom_call" | custom-call | tf_op jit(solution)/shard_map/pallas_call | solution.py:688

commit v8 on v7

--- a/solution.py
+++ b/solution.py
@@ -264,11 +264,6 @@
         )
 
     loads[0].wait()
-    for unit in range(volume):
-        coords = unit_blocks(unit, grid)[1]
-        block = green[coords[0] * size:(coords[0] + 1) * size, coords[1] * size:(coords[1] + 1) * size]
-        stage[unit] = block if unit >= paired else flipped(block)
-
     pl.semaphore_wait(barrier, inner_level + plane + has_prev + has_next)
 
     def tell(device, which):
@@ -285,11 +280,11 @@
     def span(chunk):
         return pl.ds(chunk * chunk_rows, chunk_rows)
 
-    def send_green(k):
+    def send_green(slots, k):
         peer = peer_of(k)
         unit = unit_of(peer)
         for chunk in range(CHUNKS):
-            for slot in range(2):
+            for slot in slots:
                 if slot == 0:
                     source = block_of(green, unit_blocks(unit, grid)[0], chunk * chunk_rows, chunk_rows)
                 else:
@@ -298,12 +293,18 @@
                     source, landed.at[me, slot, span(chunk)], g_send.at[chunk], g_recv.at[k, chunk], peer
                 ).start()
 
-    def send_tier(low, high):
+    def send_tier(low, high, slots=(0, 1)):
         for k in order[::-1]:
             distance = tier(peer_of(k))
-            pl.when(jnp.logical_and(distance >= low, distance <= high))(functools.partial(send_green, k))
-
-    send_tier(0, 1)
+            pl.when(jnp.logical_and(distance >= low, distance <= high))(functools.partial(send_green, slots, k))
+
+    send_tier(0, 1, (0,))
+    for unit in range(volume):
+        coords = unit_blocks(unit, grid)[1]
+        block = green[coords[0] * size:(coords[0] + 1) * size, coords[1] * size:(coords[1] + 1) * size]
+        stage[unit] = block if unit >= paired else flipped(block)
+
+    send_tier(0, 1, (1,))
     pl.semaphore_wait(ready.at[0], plane - 1)
 
     @pl.when(inner_level > 0)

time: 47.5 us -> 47.7 us (level)
  no operation moved by 1% of the time
where the time goes in v8:
time: 47.7 us; the launch traced here: 47.5 us
  Pallas kernels  47.5 us (100%)
    pallas_call x1, Pallas kernels, fused_on_device(): pl.pallas_call(functools.partial(fused_kernel, volume, slabs, grid, 0.5 /...  46 us
    pallas_call x1, Pallas kernels, fused_on_device(): pl.pallas_call(functools.partial(dress_kernel, inv_root), out_shape=jax.S...  1.51 us

profile of v8, /device:TPU:1, one launch (start us, length us, event | category | flops | bytes accessed | tf_op | source)
XLA Modules:
  0.0 47.5 jit_solution(3888414893147373624)
XLA Ops:
  0.0 46.0 %shard_map.46 = (bf16[512,512]{1,0:T(8,128)(2,1)S(1)}, bf16[512,512]{1,0:T(8,128)(2,1)S(1)}) custom-call(bf16[512,512]{1,0:T(8,128)(2,1)} %bitcast.9, bf16[512,512]{1,0:T(8,128)(2,1)} %bitcast.10, s32[8,128]{1,0:T(8,128)} %bitcast.11, bf16[8,128]{1,0:T(8,128)(2,1)} %bitcast.12), custom_call_target="tpu_custom_call" | custom-call | tf_op jit(solution)/shard_map/pallas_call | solution.py:664
  46.0 1.5 %shard_map.47 = bf16[512,512]{1,0:T(8,128)(2,1)} custom-call(bf16[512,512]{1,0:T(8,128)(2,1)S(1)} %get-tuple-element.7.total, bf16[512,512]{1,0:T(8,128)(2,1)S(1)} %get-tuple-element.8.green), custom_call_target="tpu_custom_call" | custom-call | tf_op jit(solution)/shard_map/pallas_call | solution.py:689
